TPU v7x, 32 devices: a whole 2x2x4 slice. The times are simulated.
32 devices in a mesh: gx: 16 (over z, y, core), gy: 2 (over x).
Axes of the slice: x: 2, y: 2, z: 4, core: 2. Of those that a mesh axis runs over, the one named last changes fastest.
Arguments:
- prognostic_values: float32 [3, 6, 2048, 1024], P(None, None, 'gx', 'gy'), may hold values from -6 to 6
- forcing_host_values: bfloat16 [3, 6, 2048, 1024], P(None, None, 'gx', 'gy'), may hold values from -6 to 6
- strength: float32 [3, 6], replicated, may hold values from 50 to 200
- level_height: float32 [3], replicated, may hold values from 0.2 to 3
- pbl_height: float32 [2048, 1024], P('gx', 'gy'), may hold values from 0.2 to 3
Outputs:
- tendency: bfloat16 [3, 6, 2048, 1024], P(None, None, 'gx', 'gy')
- energy: float32 [3, 6], replicated
All inputs are finite; a program needn't handle non-finite values.
Results may differ from a plain program's by a relative error of at most 0.001.
Values sent between devices are 32-bit elements; how exact they have to be, the bound alone decides.
A program may use at most 64 MiB of HBM per device.

v0:
```python
import jax
import jax.numpy as jnp
from jax import lax
from jax.sharding import PartitionSpec as P

KX = 32
KY = 32
ramp_depth = 0.25


def cosine_table(total, modes, start, count):
    index = (start + jnp.arange(count)).astype(jnp.float32)
    waves = jnp.arange(modes).astype(jnp.float32)
    scales = jnp.where(waves == 0.0, jnp.sqrt(1.0 / total), jnp.sqrt(2.0 / total)).astype(
        jnp.float32
    )
    return scales[None, :] * jnp.cos(jnp.pi * (index[:, None] + 0.5) * waves[None, :] / total)


def per_device(prognostic_values, forcing_host_values, strength, level_height, pbl_height):
    rows = prognostic_values.shape[2]
    cols = prognostic_values.shape[3]
    largest_wavenumber = lax.Precision.HIGHEST
    row_table = cosine_table(rows * lax.axis_size("gx"), KX, lax.axis_index("gx") * rows, rows)
    col_table = cosine_table(cols * lax.axis_size("gy"), KY, lax.axis_index("gy") * cols, cols)
    diff = forcing_host_values.astype(jnp.float32) - prognostic_values
    part = jnp.einsum("...ij,jb->...ib", diff, col_table, precision=largest_wavenumber)
    mode_factors = lax.psum(
        jnp.einsum("ia,...ib->...ab", row_table, part, precision=largest_wavenumber), ("gx", "gy")
    )
    restored_fields = jnp.einsum(
        "ia,lvab->lvib", row_table, mode_factors, precision=largest_wavenumber
    )
    recon = jnp.einsum("lvib,jb->lvij", restored_fields, col_table, precision=largest_wavenumber)
    damping_share = 1.0 / (
        1.0 + jnp.exp(-(level_height[:, None, None] - pbl_height[None]) / ramp_depth)
    )
    tendency = (strength[:, :, None, None] * damping_share[:, None] * recon).astype(jnp.bfloat16)
    energy = jnp.sum(mode_factors * mode_factors, axis=(2, 3)) / (KX * KY)
    return (tendency, energy)


def solution(mesh):
    return jax.shard_map(
        per_device,
        mesh=mesh,
        in_specs=(P(None, None, "gx", "gy"), P(None, None, "gx", "gy"), P(), P(), P("gx", "gy")),
        out_specs=(P(None, None, "gx", "gy"), P()),
        check_vma=False,
    )
```

profile of v0, /device:TPU:8, one launch (start us, length us, event | category | flops | bytes accessed | tf_op | source)
XLA Modules:
  0.0 161.8 jit_solution(8054716955889368383)
XLA Ops:
  7.2 0.0 copy-start
  7.2 0.0 copy-start.1
  7.2 0.0 all-reduce.2.cloned.1.call-start
  7.3 0.0 copy-start.2
  7.3 7.3 %fusion = f32[3,6,128,32]{2,3,1,0:T(8,128)S(1)} fusion(f32[3,6,128,512]{3,2,1,0:T(8,128)} %param.5, bf16[3,6,128,512]{3,2,1,0:T(8,128)(2,1)} %param.6, f32[32]{0:T(128)S(1)} %iota_convert_fusion, f32[512]{0:T(512)S(1)} %add_multiply_fusion, f32[32]{0:T(128)S(1)} %compare_select_fusion.1), kind=kOutput, calls=%fused_computation.1 | convolution fusion | flops 455393280 | bytes 7375104 | tf_op jit(solution)/shard_map/...ij,jb->...ib/dot_general | solution.py:27
  14.6 1.2 convolution_bitcast_fusion.1
  15.8 0.0 all-reduce.2.cloned.1.call-update
  15.8 0.0 copy-done
  15.9 0.0 copy-done.1
  15.9 0.3 add_divide_fusion
  16.2 129.9 %all-reduce.2.cloned.1.call-done = f32[3,6,32,32]{2,3,1,0:T(8,128)} async-done(((f32[3,6,32,32]{2,3,1,0:T(8,128)}), f32[3,6,32,32]{2,3,1,0:T(8,128)}) %all-reduce.2.cloned.1.call-update) | async-done | bytes 73744 | tf_op jit(solution)/shard_map/psum | solution.py:28
  146.0 1.1 multiply_reduce_fusion
  147.1 0.6 broadcast_multiply_fusion
  147.7 1.5 convolution_bitcast_fusion
  149.2 0.0 copy-done.2
  149.2 5.8 %multiply_convert_fusion = bf16[3,6,128,512]{3,2,1,0:T(8,128)(2,1)} fusion(f32[3,128,512]{2,1,0:T(8,128)S(1)} %add_divide_fusion, f32[3,6]{1,0:T(4,128)S(1)} %copy-done.2, f32[3,6,128,32]{2,3,1,0:T(8,128)S(1)} %convolution_bitcast_fusion, f32[32]{0:T(128)S(1)} %iota_convert_fusion, f32[512]{0:T(512)S(1)} %add_multiply_fusion, f32[32]{0:T(128)S(1)} %compare_select_fusion.1), kind=kOutput, calls=%fused_computation | convolution fusion | flops 456572928 | bytes 3443016 | tf_op jit(solution)/shard_map/lvib,jb->lvij/dot_general | solution.py:34
  (5 shorter events, 0.0 us)
Async XLA Ops:
  7.2 8.7 %copy-start = (f32[128,512]{1,0:T(8,128)S(1)}, f32[128,512]{1,0:T(8,128)}, u32[]{:S(2)}) copy-start(f32[128,512]{1,0:T(8,128)} %param.9) | copy-start | bytes 786436
  7.2 8.7 %copy-start.1 = (f32[3]{0:T(128)S(1)}, f32[3]{0:T(128)}, u32[]{:S(2)}) copy-start(f32[3]{0:T(128)} %param.8) | copy-start | bytes 40
  7.2 138.9 %all-reduce.2.cloned.1.call-start = ((), (), s32[]{:S(2)}) async-start(), calls=%async_computation | async-start | bytes 589824 | tf_op jit(solution)/shard_map/psum | solution.py:28
  7.3 141.9 %copy-start.2 = (f32[3,6]{1,0:T(4,128)S(1)}, f32[3,6]{1,0:T(4,128)}, u32[]{:S(2)}) copy-start(f32[3,6]{1,0:T(4,128)} %param.7) | copy-start | bytes 220
Sparse Core Ops, SparseCore 0:
  16.0 130.0 all-reduce.1
where the time goes:
time: 162 us
  waiting for transfers between devices  130 us (80%)
  matrix products  15.7 us (10%)
  between operations  14.1 us (9%)
  other arithmetic  2 us (1%)
    psum x1, waiting for transfers between devices, per_device(): lax.psum(jnp.einsum('ia,...ib->...ab', row_table, part, precision=largest...  130 us
    dot_general x1, matrix products, per_device(): jnp.einsum('...ij,jb->...ib', diff, col_table, precision=largest_wavenumber)  7.27 us
    dot_general x1, matrix products, per_device(): jnp.einsum('lvib,jb->lvij', restored_fields, col_table, precision=largest...  5.76 us
  transfers between devices with their start and end apart: 1, of which 1 were waited for; matrix products, arithmetic and copies ran while one was open for 0% of the time, Pallas kernels for 0%

commit v1 on v0

--- a/solution.py
+++ b/solution.py
@@ -6,6 +6,7 @@
 KX = 32
 KY = 32
 ramp_depth = 0.25
+_hold_rings = lambda tile_in, group_axis: lax.all_gather(tile_in, axis_name=group_axis).sum(axis=0)
 
 
 def cosine_table(total, modes, start, count):
@@ -25,7 +26,7 @@
     col_table = cosine_table(cols * lax.axis_size("gy"), KY, lax.axis_index("gy") * cols, cols)
     diff = forcing_host_values.astype(jnp.float32) - prognostic_values
     part = jnp.einsum("...ij,jb->...ib", diff, col_table, precision=largest_wavenumber)
-    mode_factors = lax.psum(
+    mode_factors = _hold_rings(
         jnp.einsum("ia,...ib->...ab", row_table, part, precision=largest_wavenumber), ("gx", "gy")
     )
     restored_fields = jnp.einsum(

time: 162 us -> 120 us (0.74); the launches traced: 162 us -> 118 us
  waiting for transfers between devices: 130 us -> 82.4 us
  other arithmetic: 2 us -> 5.93 us
    psum x1 -> x0, waiting for transfers between devices: 130 us -> none  [per_device(): lax.psum(jnp.einsum('ia,...ib->...ab', row_table, part, precision=largest...]
    all_gather x0 -> x1, waiting for transfers between devices: none -> 82.3 us  [lax.all_gather(tile_in, axis_name=group_axis).sum(axis=0)]
    unnamed x0 -> x1, other arithmetic: none -> 4.89 us
where the time goes in v1:
time: 120 us; the launch traced here: 118 us
  waiting for transfers between devices  82.4 us (69%)
  matrix products  14.2 us (12%)
  between operations  14.1 us (12%)
  other arithmetic  5.93 us (5%)
    all_gather x1, waiting for transfers between devices, lax.all_gather(tile_in, axis_name=group_axis).sum(axis=0)  82.3 us
    dot_general x1, matrix products, per_device(): jnp.einsum('...ij,jb->...ib', diff, col_table, precision=largest_wavenumber)  7.28 us
    dot_general x1, matrix products, per_device(): jnp.einsum('lvib,jb->lvij', restored_fields, col_table, precision=largest...  5.74 us
    unnamed x1, other arithmetic  4.89 us
  transfers between devices with their start and end apart: 1, of which 1 were waited for; matrix products, arithmetic and copies ran while one was open for 0% of the time, Pallas kernels for 0%

profile of v1, /device:TPU:8, one launch (start us, length us, event | category | flops | bytes accessed | tf_op | source)
XLA Modules:
  0.0 117.7 jit_solution(5494117906103019869)
XLA Ops:
  7.2 0.0 copy-start
  7.2 0.0 copy-start.1
  7.2 0.0 all-gather.3.cloned.1.call-start
  7.3 7.3 %fusion = f32[3,6,128,32]{2,3,1,0:T(8,128)S(1)} fusion(f32[3,6,128,512]{3,2,1,0:T(8,128)} %param.5, bf16[3,6,128,512]{3,2,1,0:T(8,128)(2,1)} %param.6, f32[32]{0:T(128)S(1)} %iota_convert_fusion, f32[512]{0:T(512)S(1)} %add_multiply_fusion, f32[32]{0:T(128)S(1)} %compare_select_fusion.1), kind=kOutput, calls=%fused_computation.1 | convolution fusion | flops 455393280 | bytes 7375104 | tf_op jit(solution)/shard_map/...ij,jb->...ib/dot_general | solution.py:28
  14.6 0.5 convolution_bitcast_fusion.1
  15.1 0.9 copy.7
  16.0 0.0 all-gather.3.cloned.1.call-update
  16.0 0.0 copy-done
  16.0 0.0 copy-done.1
  16.0 0.3 add_divide_fusion
  16.3 82.3 %all-gather.3.cloned.1.call-done = f32[96,6,32,32]{3,2,1,0:T(8,128)} async-done(((f32[3,6,32,32]{3,2,1,0:T(8,128)}), f32[96,6,32,32]{3,2,1,0:T(8,128)}) %all-gather.3.cloned.1.call-update) | async-done | bytes 2359312 | tf_op jit(solution)/shard_map/all_gather | solution.py:9
  98.6 0.0 copy-start.2
  98.6 4.9 %reduce_sum.18 = f32[3,6,32,32]{3,2,1,0:T(8,128)S(1)} reduce(f32[32,3,6,32,32]{4,3,2,1,0:T(8,128)} %bitcast.22, f32[]{:T(128)} %constant.16.clone.1), dimensions={0}, to_apply=%region_0.1 | reduce | flops 571392 | bytes 2433028
  103.5 0.7 convolution_bitcast_fusion
  104.2 0.1 copy.11
  104.4 0.1 multiply_reduce_fusion
  104.5 0.6 broadcast_multiply_fusion
  105.1 0.0 copy-done.2
  105.1 5.7 %multiply_convert_fusion = bf16[3,6,128,512]{3,2,1,0:T(8,128)(2,1)} fusion(f32[3,128,512]{2,1,0:T(8,128)S(1)} %add_divide_fusion, f32[3,6]{1,0:T(4,128)S(1)} %copy-done.2, f32[3,6,128,32]{2,3,1,0:T(8,128)S(1)} %convolution_bitcast_fusion, f32[32]{0:T(128)S(1)} %iota_convert_fusion, f32[512]{0:T(512)S(1)} %add_multiply_fusion, f32[32]{0:T(128)S(1)} %compare_select_fusion.1), kind=kOutput, calls=%fused_computation | convolution fusion | flops 456572928 | bytes 3443016 | tf_op jit(solution)/shard_map/lvib,jb->lvij/dot_general | solution.py:35
  (5 shorter events, 0.0 us)
Async XLA Ops:
  7.2 8.8 %copy-start = (f32[128,512]{1,0:T(8,128)S(1)}, f32[128,512]{1,0:T(8,128)}, u32[]{:S(2)}) copy-start(f32[128,512]{1,0:T(8,128)} %param.9) | copy-start | bytes 786436
  7.2 8.8 %copy-start.1 = (f32[3]{0:T(128)S(1)}, f32[3]{0:T(128)}, u32[]{:S(2)}) copy-start(f32[3]{0:T(128)} %param.8) | copy-start | bytes 40
  7.2 91.5 %all-gather.3.cloned.1.call-start = ((), (), s32[]{:S(2)}) async-start(), calls=%async_computation | async-start | bytes 9732096 | tf_op jit(solution)/shard_map/all_gather | solution.py:9
  98.6 6.4 %copy-start.2 = (f32[3,6]{1,0:T(4,128)S(1)}, f32[3,6]{1,0:T(4,128)}, u32[]{:S(2)}) copy-start(f32[3,6]{1,0:T(4,128)} %param.7) | copy-start | bytes 220
Sparse Core Ops, SparseCore 0:
  16.1 82.4 all-gather.2
